TPU v7x, 32 devices: a whole 2x2x4 slice. The times are simulated.
32 devices in a mesh: dp: 8 (over z, y), tensor: 4 (over x, core).
Axes of the slice: x: 2, y: 2, z: 4, core: 2. Of those that a mesh axis runs over, the one named last changes fastest.
Arguments:
- block_input: bfloat16 [2, 1024, 8, 1024], P(None, 'tensor', 'dp'), may hold values from -6 to 6
- qkv_weight: bfloat16 [1024, 3, 1024], P('dp', None, 'tensor'), may hold values from -0.1875 to 0.1875
- qv_bias: float32 [2, 1024], P(None, 'tensor'), may hold values from -2 to 2
- out_weight: bfloat16 [1024, 1024], P('dp', 'tensor'), may hold values from -0.75 to 0.75
- out_bias: float32 [1024], replicated, may hold values from -2 to 2
- fc_weight: bfloat16 [1024, 4096], P('dp', 'tensor'), may hold values from -0.1875 to 0.1875
- fc_bias: float32 [4096], P('tensor'), may hold values from -2 to 2
- proj_weight: bfloat16 [1024, 4096], P('dp', 'tensor'), may hold values from -0.09375 to 0.09375
- proj_bias: float32 [1024], replicated, may hold values from -2 to 2
- norm1_gain: float32 [1024], replicated, may hold values from 0.1 to 1.9
- norm1_shift: float32 [1024], replicated, may hold values from -2 to 2
- norm2_gain: float32 [1024], replicated, may hold values from 0.1 to 1.9
- norm2_shift: float32 [1024], replicated, may hold values from -2 to 2
- out_grad: bfloat16 [2, 1024, 8, 1024], P(None, 'tensor', 'dp'), may hold values from -6 to 6
Outputs:
- block_output: bfloat16 [2, 1024, 8, 1024], P(None, 'tensor', 'dp')
- input_grad: bfloat16 [2, 1024, 8, 1024], P(None, 'tensor', 'dp')
- qkv_weight_grad: float32 [1024, 3, 1024], P('dp', None, 'tensor')
- qv_bias_grad: float32 [2, 1024], P(None, 'tensor')
- out_weight_grad: float32 [1024, 1024], P('dp', 'tensor')
- out_bias_grad: float32 [1024], replicated
- fc_weight_grad: float32 [1024, 4096], P('dp', 'tensor')
- fc_bias_grad: float32 [4096], P('tensor')
- proj_weight_grad: float32 [1024, 4096], P('dp', 'tensor')
- proj_bias_grad: float32 [1024], replicated
- norm1_gain_grad: float32 [1024], replicated
- norm1_shift_grad: float32 [1024], replicated
- norm2_gain_grad: float32 [1024], replicated
- norm2_shift_grad: float32 [1024], replicated
All inputs are finite; a program needn't handle non-finite values.
Results may differ from a plain program's by a relative error of at most 0.012.
Values may be sent and summed in bfloat16 or wider, within the bound.
A program may use at most 128 MiB of HBM per device.

v0:
```python
import jax
import jax.numpy as jnp
from jax import lax
from jax.sharding import PartitionSpec as P

HEAD_DIM = 64
norm_eps = 1e-05
tanh_coef = 0.7978845608028654
cube_coef = 0.044715
block_rows = 512


def gelu_tanh(values):
    return (
        0.5 * values * (1.0 + jnp.tanh(tanh_coef * (values + cube_coef * values * values * values)))
    )


def norm_parts(rows):
    center = rows - jnp.mean(rows, axis=-1, keepdims=True)
    spread = jnp.mean(center * center, axis=-1, keepdims=True)
    inverse = lax.rsqrt(spread + norm_eps)
    return (center * inverse, inverse)


def norm_back(grad_out, normed, inverse, gain):
    grad_normed = grad_out * gain
    first = jnp.mean(grad_normed, axis=-1, keepdims=True)
    second = jnp.mean(grad_normed * normed, axis=-1, keepdims=True)
    return inverse * (grad_normed - first - normed * second)


def causal_scores(query_block, keys, offset):
    scores = jnp.einsum(
        "qbhe,kbhe->bhqk", query_block, keys, preferred_element_type=jnp.float32
    ) * HEAD_DIM ** (-0.5)
    height = query_block.shape[0]
    length = keys.shape[0]
    row_pos = lax.broadcasted_iota(jnp.int32, (height, length), 0) + offset
    col_pos = lax.broadcasted_iota(jnp.int32, (height, length), 1)
    return jnp.where(col_pos <= row_pos, scores, -1e30)


def attend_forward(queries, keys, values):
    length = keys.shape[0]
    span = min(block_rows, length)
    outputs = []
    totals = []
    for offset in range(0, length, span):
        scores = causal_scores(queries[offset : offset + span], keys, offset)
        peak = jnp.max(scores, axis=-1, keepdims=True)
        raised = jnp.exp(scores - peak)
        total = jnp.sum(raised, axis=-1, keepdims=True)
        weights = (raised / total).astype(jnp.bfloat16)
        outputs.append(
            jnp.einsum("bhqk,kbhe->qbhe", weights, values, preferred_element_type=jnp.float32)
        )
        totals.append(peak + jnp.log(total))
    return (jnp.concatenate(outputs, 0), jnp.concatenate(totals, 2))


def attend_backward(queries, keys, values, log_totals, grad_out):
    length = keys.shape[0]
    span = min(block_rows, length)
    scale = HEAD_DIM ** (-0.5)
    grad_queries = []
    grad_keys = jnp.zeros(keys.shape, jnp.float32)
    grad_values = jnp.zeros(values.shape, jnp.float32)
    for offset in range(0, length, span):
        query_block = queries[offset : offset + span]
        grad_block = grad_out[offset : offset + span]
        scores = causal_scores(query_block, keys, offset)
        probs = jnp.exp(scores - log_totals[:, :, offset : offset + span])
        grad_probs = jnp.einsum(
            "qbhe,kbhe->bhqk", grad_block, values, preferred_element_type=jnp.float32
        )
        inner = jnp.sum(probs * grad_probs, axis=-1, keepdims=True)
        grad_scores = (probs * (grad_probs - inner)).astype(jnp.bfloat16)
        grad_queries.append(
            jnp.einsum("bhqk,kbhe->qbhe", grad_scores, keys, preferred_element_type=jnp.float32)
            * scale
        )
        grad_keys = (
            grad_keys
            + jnp.einsum(
                "bhqk,qbhe->kbhe", grad_scores, query_block, preferred_element_type=jnp.float32
            )
            * scale
        )
        grad_values = grad_values + jnp.einsum(
            "bhqk,qbhe->kbhe",
            probs.astype(jnp.bfloat16),
            grad_block,
            preferred_element_type=jnp.float32,
        )
    return (jnp.concatenate(grad_queries, 0), grad_keys, grad_values)


def per_device(
    block_input,
    qkv_weight,
    qv_bias,
    out_weight,
    out_bias,
    fc_weight,
    fc_bias,
    proj_weight,
    proj_bias,
    norm1_gain,
    norm1_shift,
    norm2_gain,
    norm2_shift,
    out_grad,
):
    micro = block_input.shape[0]
    heads_local = qkv_weight.shape[2] // HEAD_DIM
    rows = qkv_weight.shape[0]
    width_qkv = qkv_weight.shape[1] * qkv_weight.shape[2]
    width_out = out_weight.shape[1]
    width_fc = fc_weight.shape[1]
    cuts = (width_qkv, width_qkv + width_out, width_qkv + width_out + width_fc)
    packed = jnp.concatenate(
        [qkv_weight.reshape(rows, width_qkv), out_weight, fc_weight, proj_weight], axis=1
    )
    packed_full = lax.all_gather(packed, "dp", axis=0, tiled=True)
    depth = packed_full.shape[0]
    qkv_full = packed_full[:, : cuts[0]].reshape(depth, 3, qkv_weight.shape[2])
    out_full = packed_full[:, cuts[0] : cuts[1]]
    fc_full = packed_full[:, cuts[1] : cuts[2]]
    proj_full = packed_full[:, cuts[2] :]
    grad_top_all = lax.all_gather(out_grad, "tensor", axis=1, tiled=True)
    weight_init = jnp.zeros(packed_full.shape, jnp.float32)
    small_init = (
        jnp.zeros(qv_bias.shape, jnp.float32),
        jnp.zeros(fc_bias.shape, jnp.float32),
        jnp.zeros(out_bias.shape, jnp.float32),
        jnp.zeros(proj_bias.shape, jnp.float32),
        jnp.zeros(norm1_gain.shape, jnp.float32),
        jnp.zeros(norm1_shift.shape, jnp.float32),
        jnp.zeros(norm2_gain.shape, jnp.float32),
        jnp.zeros(norm2_shift.shape, jnp.float32),
    )
    outputs_init = jnp.zeros(block_input.shape, jnp.bfloat16)
    in_grads_init = jnp.zeros(block_input.shape, jnp.bfloat16)

    def one_micro(index, carry):
        outputs_all, in_grads_all, weight_acc, small_acc = carry
        resid_in = lax.dynamic_index_in_dim(block_input, index, 0, keepdims=False).astype(
            jnp.float32
        )
        grad_top = lax.dynamic_index_in_dim(out_grad, index, 0, keepdims=False)
        grad_top_full = lax.dynamic_index_in_dim(grad_top_all, index, 0, keepdims=False)
        normed1, inverse1 = norm_parts(resid_in)
        hidden1 = (normed1 * norm1_gain + norm1_shift).astype(jnp.bfloat16)
        hidden1_full = lax.all_gather(hidden1, "tensor", axis=0, tiled=True)
        length = hidden1_full.shape[0]
        batch = hidden1_full.shape[1]
        projected = jnp.einsum(
            "lbd,dce->lbce", hidden1_full, qkv_full, preferred_element_type=jnp.float32
        )
        qkv_bias = jnp.stack([qv_bias[0], jnp.zeros_like(qv_bias[0]), qv_bias[1]])
        qkv_values = (projected + qkv_bias).astype(jnp.bfloat16)
        split = qkv_values.reshape(length, batch, 3, heads_local, HEAD_DIM)
        queries = split[:, :, 0]
        keys = split[:, :, 1]
        values = split[:, :, 2]
        attended, log_totals = attend_forward(queries, keys, values)
        mixed = attended.astype(jnp.bfloat16).reshape(length, batch, heads_local * HEAD_DIM)
        attn_branch = lax.psum_scatter(
            jnp.einsum("lbi,oi->lbo", mixed, out_full, preferred_element_type=jnp.float32),
            "tensor",
            scatter_dimension=0,
            tiled=True,
        )
        middle = resid_in + attn_branch + out_bias
        normed2, inverse2 = norm_parts(middle)
        hidden2 = (normed2 * norm2_gain + norm2_shift).astype(jnp.bfloat16)
        hidden2_full = lax.all_gather(hidden2, "tensor", axis=0, tiled=True)
        pre_act = (
            jnp.einsum("lbd,df->lbf", hidden2_full, fc_full, preferred_element_type=jnp.float32)
            + fc_bias
        )
        activated = gelu_tanh(pre_act).astype(jnp.bfloat16)
        mlp_branch = lax.psum_scatter(
            jnp.einsum(
                "lbf,of->lbo", activated, proj_full, preferred_element_type=jnp.float32
            ).astype(jnp.bfloat16),
            "tensor",
            scatter_dimension=0,
            tiled=True,
        ).astype(jnp.float32)
        block_out = (middle + mlp_branch + proj_bias).astype(jnp.bfloat16)
        grad_proj = jnp.einsum(
            "lbo,lbf->of", grad_top_full, activated, preferred_element_type=jnp.float32
        )
        grad_act = jnp.einsum(
            "lbo,of->lbf", grad_top_full, proj_full, preferred_element_type=jnp.float32
        )
        _, gelu_pull = jax.vjp(gelu_tanh, pre_act)
        grad_pre = gelu_pull(grad_act)[0].astype(jnp.bfloat16)
        grad_fc_bias = jnp.sum(grad_pre.astype(jnp.float32), axis=(0, 1))
        grad_fc = jnp.einsum(
            "lbd,lbf->df", hidden2_full, grad_pre, preferred_element_type=jnp.float32
        )
        grad_h2 = lax.psum_scatter(
            jnp.einsum("lbf,df->lbd", grad_pre, fc_full, preferred_element_type=jnp.float32),
            "tensor",
            scatter_dimension=0,
            tiled=True,
        )
        grad_gain2 = jnp.sum(grad_h2 * normed2, axis=(0, 1))
        grad_shift2 = jnp.sum(grad_h2, axis=(0, 1))
        grad_mid = grad_top.astype(jnp.float32) + norm_back(grad_h2, normed2, inverse2, norm2_gain)
        grad_out_bias = jnp.sum(grad_mid, axis=(0, 1))
        grad_proj_bias = jnp.sum(grad_top.astype(jnp.float32), axis=(0, 1))
        grad_mid_full = lax.all_gather(grad_mid.astype(jnp.bfloat16), "tensor", axis=0, tiled=True)
        grad_out_w = jnp.einsum(
            "lbo,lbi->oi", grad_mid_full, mixed, preferred_element_type=jnp.float32
        )
        grad_mixed = jnp.einsum(
            "lbo,oi->lbi", grad_mid_full, out_full, preferred_element_type=jnp.float32
        )
        grad_mixed = grad_mixed.astype(jnp.bfloat16).reshape(length, batch, heads_local, HEAD_DIM)
        grad_queries, grad_keys, grad_values = attend_backward(
            queries, keys, values, log_totals, grad_mixed
        )
        grad_qkv = jnp.stack([grad_queries, grad_keys, grad_values], axis=2).astype(jnp.bfloat16)
        grad_qkv = grad_qkv.reshape(length, batch, 3, heads_local * HEAD_DIM)
        kind_sums = jnp.sum(grad_qkv.astype(jnp.float32), axis=(0, 1))
        grad_qv_bias = jnp.stack([kind_sums[0], kind_sums[2]])
        grad_qkv_w = jnp.einsum(
            "lbd,lbce->dce", hidden1_full, grad_qkv, preferred_element_type=jnp.float32
        )
        grad_h1 = lax.psum_scatter(
            jnp.einsum("lbce,dce->lbd", grad_qkv, qkv_full, preferred_element_type=jnp.float32),
            "tensor",
            scatter_dimension=0,
            tiled=True,
        )
        grad_gain1 = jnp.sum(grad_h1 * normed1, axis=(0, 1))
        grad_shift1 = jnp.sum(grad_h1, axis=(0, 1))
        grad_in = (grad_mid + norm_back(grad_h1, normed1, inverse1, norm1_gain)).astype(
            jnp.bfloat16
        )
        fresh_weights = jnp.concatenate(
            [grad_qkv_w.reshape(depth, width_qkv), grad_out_w, grad_fc, grad_proj], axis=1
        )
        weight_acc = weight_acc + fresh_weights
        fresh = (
            grad_qv_bias,
            grad_fc_bias,
            grad_out_bias,
            grad_proj_bias,
            grad_gain1,
            grad_shift1,
            grad_gain2,
            grad_shift2,
        )
        small_acc = tuple((total + extra for total, extra in zip(small_acc, fresh)))
        outputs_all = lax.dynamic_update_index_in_dim(outputs_all, block_out, index, 0)
        in_grads_all = lax.dynamic_update_index_in_dim(in_grads_all, grad_in, index, 0)
        return (outputs_all, in_grads_all, weight_acc, small_acc)

    outputs_all, in_grads_all, weight_acc, small_acc = lax.fori_loop(
        0, micro, one_micro, (outputs_init, in_grads_init, weight_init, small_init)
    )
    weight_shard = lax.psum_scatter(weight_acc, "dp", scatter_dimension=0, tiled=True)
    grad_qkv_w = weight_shard[:, : cuts[0]].reshape(qkv_weight.shape)
    grad_out_w = weight_shard[:, cuts[0] : cuts[1]]
    grad_fc_w = weight_shard[:, cuts[1] : cuts[2]]
    grad_proj_w = weight_shard[:, cuts[2] :]
    tensor_size = lax.psum(1, "tensor")
    slot = lax.axis_index("tensor")
    head_vec = jnp.concatenate([small_acc[0].reshape(-1), small_acc[1]])
    head_slots = jnp.zeros((tensor_size, head_vec.shape[0]), jnp.float32)
    head_slots = lax.dynamic_update_index_in_dim(head_slots, head_vec, slot, 0)
    feature_vec = jnp.concatenate([item for item in small_acc[2:]])
    total = lax.psum(jnp.concatenate([feature_vec, head_slots.reshape(-1)]), ("dp", "tensor"))
    features = total[: feature_vec.shape[0]].reshape(6, -1)
    head_total = lax.dynamic_index_in_dim(
        total[feature_vec.shape[0] :].reshape(tensor_size, -1), slot, 0, keepdims=False
    )
    qv_size = small_acc[0].size
    grad_qv_bias = head_total[:qv_size].reshape(small_acc[0].shape)
    grad_fc_bias = head_total[qv_size:]
    return (
        outputs_all,
        in_grads_all,
        grad_qkv_w,
        grad_qv_bias,
        grad_out_w,
        features[0],
        grad_fc_w,
        grad_fc_bias,
        grad_proj_w,
        features[1],
        features[2],
        features[3],
        features[4],
        features[5],
    )


def solution(mesh):
    in_specs = (
        P(None, "tensor", "dp", None),
        P("dp", None, "tensor"),
        P(None, "tensor"),
        P("dp", "tensor"),
        P(),
        P("dp", "tensor"),
        P("tensor"),
        P("dp", "tensor"),
        P(),
        P(),
        P(),
        P(),
        P(),
        P(None, "tensor", "dp", None),
    )
    out_specs = (
        P(None, "tensor", "dp", None),
        P(None, "tensor", "dp", None),
        P("dp", None, "tensor"),
        P(None, "tensor"),
        P("dp", "tensor"),
        P(),
        P("dp", "tensor"),
        P("tensor"),
        P("dp", "tensor"),
        P(),
        P(),
        P(),
        P(),
        P(),
    )
    return jax.shard_map(
        per_device, mesh=mesh, in_specs=in_specs, out_specs=out_specs, check_vma=False
    )
```

profile of v0, /device:TPU:0, one launch (start us, length us, event | category | flops | bytes accessed | tf_op | source)
XLA Modules:
  0.0 999.4 jit_solution(10423390227295797122)
XLA Ops:
  13.4 101.5 %all-gather.6.cloned.1.call-done = bf16[1024,3072]{0,1:T(8,128)(2,1)} async-done(((bf16[128,3072]{0,1:T(8,128)(2,1)}), bf16[1024,3072]{0,1:T(8,128)(2,1)}) %all-gather.6.cloned.1.call-update) | async-done | bytes 6291472 | tf_op jit(solution)/shard_map/all_gather | solution.py:125
  130.1 19.0 %all-gather.8.cloned.1.call-done = bf16[2,1024,1,1024]{3,1,2,0:T(8,128)(2,1)} async-done(((bf16[2,256,1,1024]{3,1,2,0:T(8,128)(2,1)}), bf16[2,1024,1,1024]{3,1,2,0:T(8,128)(2,1)}) %all-gather.8.cloned.1.call-update) | async-done | bytes 4194320 | tf_op jit(solution)/shard_map/all_gather | solution.py:131
  149.1 623.7 %while.34 = (s32[]{:T(128)}, bf16[2,256,1,1024]{3,1,2,0:T(8,128)(2,1)}, bf16[2,256,1,1024]{3,1,2,0:T(8,128)(2,1)}, f32[1024,3072]{0,1:T(8,128)}, f32[2,256]{1,0:...) while((s32[]{:T(128)}, ...), condition=%wide.region_27.28_spmd.clone, body=%wide.region_0.27_spmd.clone.sunk | while | flops 22718711808 | bytes 744419392 | solution.py:264
  151.7 23.2 %all-gather.10.cloned.1.call-done = bf16[1024,1,1024]{2,0,1:T(8,128)(2,1)} async-done(((bf16[256,1,1024]{2,0,1:T(8,128)(2,1)}), bf16[1024,1,1024]{2,0,1:T(8,128)(2,1)}) %all-gather.10.cloned.1.call-update) | async-done | bytes 2097168 | tf_op jit(solution)/shard_map/while/body/eval_jaxpr/all_gather | solution.py:155
  196.7 44.7 %reduce-scatter.8.cloned.1.call-done = f32[256,1,1024]{2,0,1:T(8,128)} async-done(((f32[1024,1,1024]{2,0,1:T(8,128)}), f32[256,1,1024]{2,0,1:T(8,128)}) %reduce-scatter.8.cloned.1.call-update) | async-done | bytes 1048592 | tf_op jit(solution)/shard_map/while/body/eval_jaxpr/reduce_scatter | solution.py:169
  244.5 22.4 %all-gather.12.cloned.1.call-done = bf16[1024,1,1024]{2,0,1:T(8,128)(2,1)} async-done(((bf16[256,1,1024]{2,0,1:T(8,128)(2,1)}), bf16[1024,1,1024]{2,0,1:T(8,128)(2,1)}) %all-gather.12.cloned.1.call-update) | async-done | bytes 2097168 | tf_op jit(solution)/shard_map/while/body/eval_jaxpr/all_gather | solution.py:178
  271.6 5.7 convert_reduce_fusion.9
  283.1 44.7 %reduce-scatter.12.cloned.1.call-done = f32[256,1,1024]{2,0,1:T(8,128)} async-done(((f32[1024,1,1024]{2,0,1:T(8,128)}), f32[256,1,1024]{2,0,1:T(8,128)}) %reduce-scatter.12.cloned.1.call-update) | async-done | bytes 1048592 | tf_op jit(solution)/shard_map/while/body/eval_jaxpr/reduce_scatter | solution.py:205
  332.3 7.0 convert_bitcast_fusion.4
  339.8 15.1 %all-gather.14.cloned.1.call-done = bf16[1024,1,1024]{2,0,1:T(8,128)(2,1)} async-done(((bf16[256,1,1024]{2,0,1:T(8,128)(2,1)}), bf16[1024,1,1024]{2,0,1:T(8,128)(2,1)}) %all-gather.14.cloned.1.call-update) | async-done | bytes 2097168 | tf_op jit(solution)/shard_map/while/body/eval_jaxpr/all_gather | solution.py:216
  362.4 7.6 multiply_reduce_fusion.13
  374.6 6.8 multiply_convert_fusion.11
  384.3 5.5 multiply_reduce_fusion.14
  405.1 5.7 convolution_bitcast_fusion.8
  411.9 6.7 fusion.227
  438.5 5.7 maximum_add_fusion.4
  444.2 11.6 %reduce-scatter.14.cloned.1.call-done = f32[256,1,1024]{2,0,1:T(8,128)} async-done(((f32[1024,1,1024]{2,0,1:T(8,128)}), f32[256,1,1024]{2,0,1:T(8,128)}) %reduce-scatter.14.cloned.1.call-update) | async-done | bytes 1048592 | tf_op jit(solution)/shard_map/while/body/eval_jaxpr/reduce_scatter | solution.py:234
  462.6 22.9 %all-gather.10.cloned.1.call-done = bf16[1024,1,1024]{2,0,1:T(8,128)(2,1)} async-done(((bf16[256,1,1024]{2,0,1:T(8,128)(2,1)}), bf16[1024,1,1024]{2,0,1:T(8,128)(2,1)}) %all-gather.10.cloned.1.call-update) | async-done | bytes 2097168 | tf_op jit(solution)/shard_map/while/body/eval_jaxpr/all_gather | solution.py:155
  507.3 44.7 %reduce-scatter.8.cloned.1.call-done = f32[256,1,1024]{2,0,1:T(8,128)} async-done(((f32[1024,1,1024]{2,0,1:T(8,128)}), f32[256,1,1024]{2,0,1:T(8,128)}) %reduce-scatter.8.cloned.1.call-update) | async-done | bytes 1048592 | tf_op jit(solution)/shard_map/while/body/eval_jaxpr/reduce_scatter | solution.py:169
  555.3 22.2 %all-gather.12.cloned.1.call-done = bf16[1024,1,1024]{2,0,1:T(8,128)(2,1)} async-done(((bf16[256,1,1024]{2,0,1:T(8,128)(2,1)}), bf16[1024,1,1024]{2,0,1:T(8,128)(2,1)}) %all-gather.12.cloned.1.call-update) | async-done | bytes 2097168 | tf_op jit(solution)/shard_map/while/body/eval_jaxpr/all_gather | solution.py:178
  582.2 5.7 convert_reduce_fusion.9
  593.7 44.7 %reduce-scatter.12.cloned.1.call-done = f32[256,1,1024]{2,0,1:T(8,128)} async-done(((f32[1024,1,1024]{2,0,1:T(8,128)}), f32[256,1,1024]{2,0,1:T(8,128)}) %reduce-scatter.12.cloned.1.call-update) | async-done | bytes 1048592 | tf_op jit(solution)/shard_map/while/body/eval_jaxpr/reduce_scatter | solution.py:205
  642.9 7.0 convert_bitcast_fusion.4
  650.1 15.4 %all-gather.14.cloned.1.call-done = bf16[1024,1,1024]{2,0,1:T(8,128)(2,1)} async-done(((bf16[256,1,1024]{2,0,1:T(8,128)(2,1)}), bf16[1024,1,1024]{2,0,1:T(8,128)(2,1)}) %all-gather.14.cloned.1.call-update) | async-done | bytes 2097168 | tf_op jit(solution)/shard_map/while/body/eval_jaxpr/all_gather | solution.py:216
  673.0 7.6 multiply_reduce_fusion.13
  685.1 6.8 multiply_convert_fusion.11
  715.7 5.7 convolution_bitcast_fusion.8
  722.5 6.7 fusion.227
  749.2 10.1 %maximum_add_fusion.4 = f32[1024,3072]{0,1:T(8,128)} fusion(f32[1024,1024]{0,1:T(8,128)S(1)} %copy-done.11, f32[1024,1024]{0,1:T(8,128)S(1)} %copy-done.10, f32[1024,256]{0,1:T(8,128)S(1)} %fusion.228, f32[1024,768]{0,1:T(8,128)S(1)} %fusion.230, f32[1024,3072]{0,1:T(8,128)} %get-tuple-element.947, pred[]{:T(512)S(6)} %compare.3), kind=kLoop, calls=%fused_computation.clone.1 | loop fusion | flops 15728640 | bytes 37748736 | tf_op jit(solution)/shard_map/while/body/eval_jaxpr/add | solution.py:248
  759.3 7.1 reduce-scatter.14.cloned.1.call-done
  773.7 43.1 %psum.7 = f32[12288]{0:T(1024)S(1)} all-reduce(f32[12288]{0:T(1024)S(1)} %constant_dynamic-update-slice_fusion), channel_id=1, replica_groups=mesh['dp'=8,'tensor'=4] {'dp','tensor'}, use_global_device_ids=true, to_apply=%region_29.30 | all-reduce | flops 12288 | bytes 98304 | tf_op jit(solution)/shard_map/psum | solution.py:278
  818.7 167.7 %reduce-scatter.6.cloned.1.call-done = f32[128,3072]{0,1:T(8,128)} async-done(((f32[1024,3072]{0,1:T(8,128)}), f32[128,3072]{0,1:T(8,128)}) %reduce-scatter.6.cloned.1.call-update) | async-done | bytes 1572880 | tf_op jit(solution)/shard_map/reduce_scatter | solution.py:267
  (354 shorter events, 230.4 us)
Async XLA Ops:
  7.2 107.7 %all-gather.6.cloned.1.call-start = ((), (), s32[]{:S(2)}) async-start(), calls=%async_computation.5 | async-start | bytes 7077888 | tf_op jit(solution)/shard_map/all_gather | solution.py:125
  12.5 136.6 %all-gather.8.cloned.1.call-start = ((), (), s32[]{:S(2)}) async-start(), calls=%async_computation.6 | async-start | bytes 5242880 | tf_op jit(solution)/shard_map/all_gather | solution.py:131
  122.7 26.3 %copy-start.5 = (bf16[2,256,1,1024]{3,1,2,0:T(8,128)(2,1)S(1)}, bf16[2,256,1,1024]{3,1,2,0:T(8,128)(2,1)}, u32[]{:S(2)}) copy-start(bf16[2,256,1,1024]{3,1,2,0:T(8,128)(2,1)} %param.16) | copy-start | bytes 3145732
  122.7 26.3 %copy-start.20 = (f32[1024]{0:T(1024)S(1)}, f32[1024]{0:T(1024)}, u32[]{:S(2)}) copy-start(f32[1024]{0:T(1024)} %param.25) | copy-start | bytes 12292
  122.7 26.3 %copy-start.21 = (f32[1024]{0:T(1024)S(1)}, f32[1024]{0:T(1024)}, u32[]{:S(2)}) copy-start(f32[1024]{0:T(1024)} %param.27) | copy-start | bytes 12292
  122.7 26.3 %copy-start.22 = (f32[1024]{0:T(1024)S(1)}, f32[1024]{0:T(1024)}, u32[]{:S(2)}) copy-start(f32[1024]{0:T(1024)} %param.26) | copy-start | bytes 12292
  122.8 26.3 %copy-start.23 = (f32[1024]{0:T(1024)S(1)}, f32[1024]{0:T(1024)}, u32[]{:S(2)}) copy-start(f32[1024]{0:T(1024)} %param.20) | copy-start | bytes 12292
  122.8 26.3 %copy-start.24 = (f32[1024]{0:T(1024)S(1)}, f32[1024]{0:T(1024)}, u32[]{:S(2)}) copy-start(f32[1024]{0:T(1024)} %param.28) | copy-start | bytes 12292
  122.8 26.3 %copy-start.25 = (f32[1024]{0:T(1024)S(1)}, f32[1024]{0:T(1024)}, u32[]{:S(2)}) copy-start(f32[1024]{0:T(1024)} %param.24) | copy-start | bytes 12292
  122.8 26.3 %copy-start.26 = (f32[2,256]{1,0:T(2,128)S(1)}, f32[2,256]{1,0:T(2,128)}, u32[]{:S(2)}) copy-start(f32[2,256]{1,0:T(2,128)} %param.18) | copy-start | bytes 6148
  122.8 26.3 %copy-start.30 = (f32[1024]{0:T(1024)S(1)}, f32[1024]{0:T(1024)}, u32[]{:S(2)}) copy-start(f32[1024]{0:T(1024)} %param.22) | copy-start | bytes 12292
  149.4 43.9 %copy-start.16 = (bf16[1024,256]{1,0:T(8,128)(2,1)}, bf16[1024,256]{1,0:T(8,128)(2,1)S(1)}, u32[]{:S(2)}) copy-start(bf16[1024,256]{1,0:T(8,128)(2,1)S(1)} %get-tuple-element.992) | copy-start | bytes 1572868 | tf_op jit(solution)/shard_map/while
  149.4 25.5 %all-gather.10.cloned.1.call-start = ((), (), s32[]{:S(2)}) async-start(), calls=%async_computation.8 | async-start | bytes 2621440 | tf_op jit(solution)/shard_map/while/body/eval_jaxpr/all_gather | solution.py:155
  151.0 90.4 %reduce-scatter.8.cloned.1.call-start = ((), (), s32[]{:S(2)}) async-start(), calls=%async_computation.9 | async-start | bytes 5242880 | tf_op jit(solution)/shard_map/while/body/eval_jaxpr/reduce_scatter | solution.py:169
  196.6 70.3 %all-gather.12.cloned.1.call-start = ((), (), s32[]{:S(2)}) async-start(), calls=%async_computation.10 | async-start | bytes 2621440 | tf_op jit(solution)/shard_map/while/body/eval_jaxpr/all_gather | solution.py:178
  244.1 83.6 %reduce-scatter.12.cloned.1.call-start = ((), (), s32[]{:S(2)}) async-start(), calls=%async_computation.12 | async-start | bytes 5242880 | tf_op jit(solution)/shard_map/while/body/eval_jaxpr/reduce_scatter | solution.py:205
  283.0 71.9 %all-gather.14.cloned.1.call-start = ((), (), s32[]{:S(2)}) async-start(), calls=%async_computation.13 | async-start | bytes 2621440 | tf_op jit(solution)/shard_map/while/body/eval_jaxpr/all_gather | solution.py:216
  332.2 91.3 %reduce-scatter.10.cloned.1.call-start = ((), (), s32[]{:S(2)}) async-start(), calls=%async_computation.11 | async-start | bytes 2621440 | tf_op jit(solution)/shard_map/while/body/eval_jaxpr/reduce_scatter | solution.py:184
  339.3 116.5 %reduce-scatter.14.cloned.1.call-start = ((), (), s32[]{:S(2)}) async-start(), calls=%async_computation.14 | async-start | bytes 5242880 | tf_op jit(solution)/shard_map/while/body/eval_jaxpr/reduce_scatter | solution.py:234
  357.4 12.7 %slice-start.2 = ((s8[8388608]{0:T(1024)(128)(4,1)}), s8[4194304]{0:T(1024)(128)(4,1)S(1)}, s32[]{:S(2)}) async-start(s8[8388608]{0:T(1024)(128)(4,1)} %bitcast.324), calls=%async_computation.17 | async-start | bytes 8388608 | tf_op jit(solution)/shard_map/while
  444.2 15.8 %copy-start.17 = (bf16[1024,256]{1,0:T(8,128)(2,1)S(1)}, bf16[1024,256]{1,0:T(8,128)(2,1)}, u32[]{:S(2)}) copy-start(bf16[1024,256]{1,0:T(8,128)(2,1)} %copy-done.16) | copy-start | bytes 1572868 | tf_op jit(solution)/shard_map/while
  460.3 43.6 %copy-start.16 = (bf16[1024,256]{1,0:T(8,128)(2,1)}, bf16[1024,256]{1,0:T(8,128)(2,1)S(1)}, u32[]{:S(2)}) copy-start(bf16[1024,256]{1,0:T(8,128)(2,1)S(1)} %get-tuple-element.992) | copy-start | bytes 1572868 | tf_op jit(solution)/shard_map/while
  460.3 25.2 %all-gather.10.cloned.1.call-start = ((), (), s32[]{:S(2)}) async-start(), calls=%async_computation.8 | async-start | bytes 2621440 | tf_op jit(solution)/shard_map/while/body/eval_jaxpr/all_gather | solution.py:155
  461.9 90.1 %reduce-scatter.8.cloned.1.call-start = ((), (), s32[]{:S(2)}) async-start(), calls=%async_computation.9 | async-start | bytes 5242880 | tf_op jit(solution)/shard_map/while/body/eval_jaxpr/reduce_scatter | solution.py:169
  507.2 70.3 %all-gather.12.cloned.1.call-start = ((), (), s32[]{:S(2)}) async-start(), calls=%async_computation.10 | async-start | bytes 2621440 | tf_op jit(solution)/shard_map/while/body/eval_jaxpr/all_gather | solution.py:178
  554.8 83.6 %reduce-scatter.12.cloned.1.call-start = ((), (), s32[]{:S(2)}) async-start(), calls=%async_computation.12 | async-start | bytes 5242880 | tf_op jit(solution)/shard_map/while/body/eval_jaxpr/reduce_scatter | solution.py:205
  593.6 71.9 %all-gather.14.cloned.1.call-start = ((), (), s32[]{:S(2)}) async-start(), calls=%async_computation.13 | async-start | bytes 2621440 | tf_op jit(solution)/shard_map/while/body/eval_jaxpr/all_gather | solution.py:216
  642.8 91.3 %reduce-scatter.10.cloned.1.call-start = ((), (), s32[]{:S(2)}) async-start(), calls=%async_computation.11 | async-start | bytes 2621440 | tf_op jit(solution)/shard_map/while/body/eval_jaxpr/reduce_scatter | solution.py:184
  649.9 116.5 %reduce-scatter.14.cloned.1.call-start = ((), (), s32[]{:S(2)}) async-start(), calls=%async_computation.14 | async-start | bytes 5242880 | tf_op jit(solution)/shard_map/while/body/eval_jaxpr/reduce_scatter | solution.py:234
  668.0 12.7 %slice-start.2 = ((s8[8388608]{0:T(1024)(128)(4,1)}), s8[4194304]{0:T(1024)(128)(4,1)S(1)}, s32[]{:S(2)}) async-start(s8[8388608]{0:T(1024)(128)(4,1)} %bitcast.324), calls=%async_computation.17 | async-start | bytes 8388608 | tf_op jit(solution)/shard_map/while
  759.3 11.3 %copy-start.17 = (bf16[1024,256]{1,0:T(8,128)(2,1)S(1)}, bf16[1024,256]{1,0:T(8,128)(2,1)}, u32[]{:S(2)}) copy-start(bf16[1024,256]{1,0:T(8,128)(2,1)} %copy-done.16) | copy-start | bytes 1572868 | tf_op jit(solution)/shard_map/while
  772.8 213.5 %reduce-scatter.6.cloned.1.call-start = ((), (), s32[]{:S(2)}) async-start(), calls=%async_computation.7 | async-start | bytes 14155776 | tf_op jit(solution)/shard_map/reduce_scatter | solution.py:267
  (54 other events, 267.1 us)
Sparse Core Ops, SparseCore 0:
  12.6 102.1 all-gather.5
  116.4 32.6 all-gather.7
  152.3 22.5 all-gather.9
  196.7 44.5 reduce-scatter.7
  244.3 22.5 all-gather.11
  283.1 44.5 reduce-scatter.11
  332.3 22.5 all-gather.13
  357.4 31.1 reduce-scatter.9
  410.9 44.8 reduce-scatter.13
  462.9 22.5 all-gather.9
  507.3 44.5 reduce-scatter.7
  554.9 22.5 all-gather.11
  593.7 44.5 reduce-scatter.11
  642.9 22.5 all-gather.13
  667.9 31.1 reduce-scatter.9
  721.5 44.8 reduce-scatter.13
  776.9 209.3 reduce-scatter.5
where the time goes:
time: 1000 us; the launch traced here: 999 us
  waiting for transfers between devices  608 us (61%)
  matrix products  180 us (18%)
  other arithmetic  85.3 us (9%)
  local copies, waits for them, and re-layouts  62.5 us (6%)
  blocking collectives  43.1 us (4%)
  between operations  14.7 us (1%)
    reduce_scatter x1, waiting for transfers between devices, per_device(): lax.psum_scatter(weight_acc, 'dp', scatter_dimension=0, tiled=True)  168 us
    all_gather x1, waiting for transfers between devices, per_device(): packed_full = lax.all_gather(packed, 'dp', axis=0, tiled=True)  101 us
    reduce_scatter x2, waiting for transfers between devices, one_micro(): lax.psum_scatter(jnp.einsum('lbi,oi->lbo', mixed, out_full, preferred_ele...  89.4 us
    reduce_scatter x2, waiting for transfers between devices, one_micro(): lax.psum_scatter(jnp.einsum('lbf,df->lbd', grad_pre, fc_full, preferred_e...  89.3 us
    all_gather x2, waiting for transfers between devices, one_micro(): hidden1_full = lax.all_gather(hidden1, 'tensor', axis=0, tiled=True)  46.1 us
    all_gather x2, waiting for transfers between devices, one_micro(): hidden2_full = lax.all_gather(hidden2, 'tensor', axis=0, tiled=True)  44.6 us
    psum x1, blocking collectives, per_device(): lax.psum(jnp.concatenate([feature_vec, head_slots.reshape(-1)]), ('dp', '...  43.1 us
    all_gather x2, waiting for transfers between devices, one_micro(): lax.all_gather(grad_mid.astype(jnp.bfloat16), 'tensor', axis=0, tiled=True)  30.5 us
  transfers between devices with their start and end apart: 17, of which 15 were waited for; matrix products, arithmetic and copies ran while one was open for 21% of the time, Pallas kernels for 0%

commit v1 on v0

--- a/solution.py
+++ b/solution.py
@@ -275,7 +275,9 @@
     head_slots = jnp.zeros((tensor_size, head_vec.shape[0]), jnp.float32)
     head_slots = lax.dynamic_update_index_in_dim(head_slots, head_vec, slot, 0)
     feature_vec = jnp.concatenate([item for item in small_acc[2:]])
-    total = lax.psum(jnp.concatenate([feature_vec, head_slots.reshape(-1)]), ("dp", "tensor"))
+    block = jnp.concatenate([feature_vec, head_slots.reshape(-1)])
+    terms = lax.all_gather(block, ("dp", "tensor"))
+    total = jnp.sum(terms, axis=0)
     features = total[: feature_vec.shape[0]].reshape(6, -1)
     head_total = lax.dynamic_index_in_dim(
         total[feature_vec.shape[0] :].reshape(tensor_size, -1), slot, 0, keepdims=False

time: 1000 us -> 1060 us (1.060)
  waiting for transfers between devices: 608 us -> 704 us
  blocking collectives: 43.1 us -> 0 us
    all_gather x0 -> x1, waiting for transfers between devices: none -> 57.3 us  [per_device(): terms = lax.all_gather(block, ('dp', 'tensor'))]
    psum x1 -> x0, blocking collectives: 43.1 us -> none  [per_device(): lax.psum(jnp.concatenate([feature_vec, head_slots.reshape(-1)]), ('dp', '...]
    reduce_scatter x1, waiting for transfers between devices: 168 us -> 207 us  [per_device(): lax.psum_scatter(weight_acc, 'dp', scatter_dimension=0, tiled=True)]
  transfers between devices with their start and end apart: 17 -> 18, of which waited for: 15 -> 16; matrix products, arithmetic and copies ran while one was open for 21% -> 20% of each run, Pallas kernels for 0% -> 0%
where the time goes in v1:
time: 1060 us
  waiting for transfers between devices  704 us (66%)
  matrix products  180 us (17%)
  other arithmetic  85.4 us (8%)
  local copies, waits for them, and re-layouts  64.8 us (6%)
  between operations  15 us (1%)
    reduce_scatter x1, waiting for transfers between devices, per_device(): lax.psum_scatter(weight_acc, 'dp', scatter_dimension=0, tiled=True)  207 us
    all_gather x1, waiting for transfers between devices, per_device(): packed_full = lax.all_gather(packed, 'dp', axis=0, tiled=True)  101 us
    reduce_scatter x2, waiting for transfers between devices, one_micro(): lax.psum_scatter(jnp.einsum('lbi,oi->lbo', mixed, out_full, preferred_ele...  89.4 us
    reduce_scatter x2, waiting for transfers between devices, one_micro(): lax.psum_scatter(jnp.einsum('lbf,df->lbd', grad_pre, fc_full, preferred_e...  89.3 us
    all_gather x1, waiting for transfers between devices, per_device(): terms = lax.all_gather(block, ('dp', 'tensor'))  57.3 us
    all_gather x2, waiting for transfers between devices, one_micro(): hidden1_full = lax.all_gather(hidden1, 'tensor', axis=0, tiled=True)  46.1 us
    all_gather x2, waiting for transfers between devices, one_micro(): hidden2_full = lax.all_gather(hidden2, 'tensor', axis=0, tiled=True)  44.6 us
    all_gather x2, waiting for transfers between devices, one_micro(): lax.all_gather(grad_mid.astype(jnp.bfloat16), 'tensor', axis=0, tiled=True)  30.4 us
  transfers between devices with their start and end apart: 18, of which 16 were waited for; matrix products, arithmetic and copies ran while one was open for 20% of the time, Pallas kernels for 0%

profile of v1, /device:TPU:0, one launch (start us, length us, event | category | flops | bytes accessed | tf_op | source)
XLA Modules:
  0.0 1055.1 jit_solution(13253355546455531042)
XLA Ops:
  13.4 101.5 %all-gather.8.cloned.1.call-done = bf16[1024,3072]{0,1:T(8,128)(2,1)} async-done(((bf16[128,3072]{0,1:T(8,128)(2,1)}), bf16[1024,3072]{0,1:T(8,128)(2,1)}) %all-gather.8.cloned.1.call-update) | async-done | bytes 6291472 | tf_op jit(solution)/shard_map/all_gather | solution.py:125
  130.1 19.0 %all-gather.10.cloned.1.call-done = bf16[2,1024,1,1024]{3,1,2,0:T(8,128)(2,1)} async-done(((bf16[2,256,1,1024]{3,1,2,0:T(8,128)(2,1)}), bf16[2,1024,1,1024]{3,1,2,0:T(8,128)(2,1)}) %all-gather.10.cloned.1.call-update) | async-done | bytes 4194320 | tf_op jit(solution)/shard_map/all_gather | solution.py:131
  149.2 623.5 %while.34 = (s32[]{:T(128)}, bf16[2,256,1,1024]{3,1,2,0:T(8,128)(2,1)}, bf16[2,256,1,1024]{3,1,2,0:T(8,128)(2,1)}, f32[1024,3072]{0,1:T(8,128)}, f32[2,256]{1,0:...) while((s32[]{:T(128)}, ...), condition=%wide.region_27.28_spmd.clone, body=%wide.region_0.27_spmd.clone.sunk | while | flops 22718711808 | bytes 744419392 | solution.py:264
  151.7 23.2 %all-gather.14.cloned.1.call-done = bf16[1024,1,1024]{2,0,1:T(8,128)(2,1)} async-done(((bf16[256,1,1024]{2,0,1:T(8,128)(2,1)}), bf16[1024,1,1024]{2,0,1:T(8,128)(2,1)}) %all-gather.14.cloned.1.call-update) | async-done | bytes 2097168 | tf_op jit(solution)/shard_map/while/body/eval_jaxpr/all_gather | solution.py:155
  196.7 44.7 %reduce-scatter.8.cloned.1.call-done = f32[256,1,1024]{2,0,1:T(8,128)} async-done(((f32[1024,1,1024]{2,0,1:T(8,128)}), f32[256,1,1024]{2,0,1:T(8,128)}) %reduce-scatter.8.cloned.1.call-update) | async-done | bytes 1048592 | tf_op jit(solution)/shard_map/while/body/eval_jaxpr/reduce_scatter | solution.py:169
  244.5 22.4 %all-gather.16.cloned.1.call-done = bf16[1024,1,1024]{2,0,1:T(8,128)(2,1)} async-done(((bf16[256,1,1024]{2,0,1:T(8,128)(2,1)}), bf16[1024,1,1024]{2,0,1:T(8,128)(2,1)}) %all-gather.16.cloned.1.call-update) | async-done | bytes 2097168 | tf_op jit(solution)/shard_map/while/body/eval_jaxpr/all_gather | solution.py:178
  271.7 5.7 convert_reduce_fusion.9
  283.1 44.7 %reduce-scatter.12.cloned.1.call-done = f32[256,1,1024]{2,0,1:T(8,128)} async-done(((f32[1024,1,1024]{2,0,1:T(8,128)}), f32[256,1,1024]{2,0,1:T(8,128)}) %reduce-scatter.12.cloned.1.call-update) | async-done | bytes 1048592 | tf_op jit(solution)/shard_map/while/body/eval_jaxpr/reduce_scatter | solution.py:205
  332.3 7.0 convert_bitcast_fusion.4
  339.9 15.1 %all-gather.18.cloned.1.call-done = bf16[1024,1,1024]{2,0,1:T(8,128)(2,1)} async-done(((bf16[256,1,1024]{2,0,1:T(8,128)(2,1)}), bf16[1024,1,1024]{2,0,1:T(8,128)(2,1)}) %all-gather.18.cloned.1.call-update) | async-done | bytes 2097168 | tf_op jit(solution)/shard_map/while/body/eval_jaxpr/all_gather | solution.py:216
  362.5 7.6 multiply_reduce_fusion.13
  374.6 6.8 multiply_convert_fusion.11
  384.3 5.4 multiply_reduce_fusion.14
  405.0 5.6 convolution_bitcast_fusion.8
  411.9 6.7 fusion.227
  438.5 5.7 maximum_add_fusion.4
  444.2 11.5 %reduce-scatter.14.cloned.1.call-done = f32[256,1,1024]{2,0,1:T(8,128)} async-done(((f32[1024,1,1024]{2,0,1:T(8,128)}), f32[256,1,1024]{2,0,1:T(8,128)}) %reduce-scatter.14.cloned.1.call-update) | async-done | bytes 1048592 | tf_op jit(solution)/shard_map/while/body/eval_jaxpr/reduce_scatter | solution.py:234
  462.6 22.9 %all-gather.14.cloned.1.call-done = bf16[1024,1,1024]{2,0,1:T(8,128)(2,1)} async-done(((bf16[256,1,1024]{2,0,1:T(8,128)(2,1)}), bf16[1024,1,1024]{2,0,1:T(8,128)(2,1)}) %all-gather.14.cloned.1.call-update) | async-done | bytes 2097168 | tf_op jit(solution)/shard_map/while/body/eval_jaxpr/all_gather | solution.py:155
  507.3 44.7 %reduce-scatter.8.cloned.1.call-done = f32[256,1,1024]{2,0,1:T(8,128)} async-done(((f32[1024,1,1024]{2,0,1:T(8,128)}), f32[256,1,1024]{2,0,1:T(8,128)}) %reduce-scatter.8.cloned.1.call-update) | async-done | bytes 1048592 | tf_op jit(solution)/shard_map/while/body/eval_jaxpr/reduce_scatter | solution.py:169
  555.3 22.2 %all-gather.16.cloned.1.call-done = bf16[1024,1,1024]{2,0,1:T(8,128)(2,1)} async-done(((bf16[256,1,1024]{2,0,1:T(8,128)(2,1)}), bf16[1024,1,1024]{2,0,1:T(8,128)(2,1)}) %all-gather.16.cloned.1.call-update) | async-done | bytes 2097168 | tf_op jit(solution)/shard_map/while/body/eval_jaxpr/all_gather | solution.py:178
  582.2 5.7 convert_reduce_fusion.9
  593.7 44.7 %reduce-scatter.12.cloned.1.call-done = f32[256,1,1024]{2,0,1:T(8,128)} async-done(((f32[1024,1,1024]{2,0,1:T(8,128)}), f32[256,1,1024]{2,0,1:T(8,128)}) %reduce-scatter.12.cloned.1.call-update) | async-done | bytes 1048592 | tf_op jit(solution)/shard_map/while/body/eval_jaxpr/reduce_scatter | solution.py:205
  642.9 7.0 convert_bitcast_fusion.4
  650.2 15.4 %all-gather.18.cloned.1.call-done = bf16[1024,1,1024]{2,0,1:T(8,128)(2,1)} async-done(((bf16[256,1,1024]{2,0,1:T(8,128)(2,1)}), bf16[1024,1,1024]{2,0,1:T(8,128)(2,1)}) %all-gather.18.cloned.1.call-update) | async-done | bytes 2097168 | tf_op jit(solution)/shard_map/while/body/eval_jaxpr/all_gather | solution.py:216
  673.0 7.6 multiply_reduce_fusion.13
  685.2 6.8 multiply_convert_fusion.11
  715.7 5.6 convolution_bitcast_fusion.8
  722.5 6.7 fusion.227
  749.2 10.1 maximum_add_fusion.4
  759.3 7.1 reduce-scatter.14.cloned.1.call-done
  774.2 57.3 %all-gather.12.cloned.1.call-done = f32[393216]{0:T(1024)} async-done(((f32[12288]{0:T(1024)}), f32[393216]{0:T(1024)}) %all-gather.12.cloned.1.call-update) | async-done | bytes 1572880 | tf_op jit(solution)/shard_map/all_gather | solution.py:279
  835.2 206.6 %reduce-scatter.6.cloned.1.call-done = f32[128,3072]{0,1:T(8,128)} async-done(((f32[1024,3072]{0,1:T(8,128)}), f32[128,3072]{0,1:T(8,128)}) %reduce-scatter.6.cloned.1.call-update) | async-done | bytes 1572880 | tf_op jit(solution)/shard_map/reduce_scatter | solution.py:267
  (360 shorter events, 232.9 us)
Async XLA Ops:
  7.2 107.7 %all-gather.8.cloned.1.call-start = ((), (), s32[]{:S(2)}) async-start(), calls=%async_computation.5 | async-start | bytes 7077888 | tf_op jit(solution)/shard_map/all_gather | solution.py:125
  12.5 136.6 %all-gather.10.cloned.1.call-start = ((), (), s32[]{:S(2)}) async-start(), calls=%async_computation.6 | async-start | bytes 5242880 | tf_op jit(solution)/shard_map/all_gather | solution.py:131
  122.8 26.3 %copy-start.5 = (bf16[2,256,1,1024]{3,1,2,0:T(8,128)(2,1)S(1)}, bf16[2,256,1,1024]{3,1,2,0:T(8,128)(2,1)}, u32[]{:S(2)}) copy-start(bf16[2,256,1,1024]{3,1,2,0:T(8,128)(2,1)} %param.16) | copy-start | bytes 3145732
  122.8 26.3 %copy-start.20 = (f32[1024]{0:T(1024)S(1)}, f32[1024]{0:T(1024)}, u32[]{:S(2)}) copy-start(f32[1024]{0:T(1024)} %param.25) | copy-start | bytes 12292
  122.8 26.3 %copy-start.21 = (f32[1024]{0:T(1024)S(1)}, f32[1024]{0:T(1024)}, u32[]{:S(2)}) copy-start(f32[1024]{0:T(1024)} %param.27) | copy-start | bytes 12292
  122.8 26.3 %copy-start.22 = (f32[1024]{0:T(1024)S(1)}, f32[1024]{0:T(1024)}, u32[]{:S(2)}) copy-start(f32[1024]{0:T(1024)} %param.26) | copy-start | bytes 12292
  122.8 26.3 %copy-start.23 = (f32[1024]{0:T(1024)S(1)}, f32[1024]{0:T(1024)}, u32[]{:S(2)}) copy-start(f32[1024]{0:T(1024)} %param.20) | copy-start | bytes 12292
  122.8 26.3 %copy-start.24 = (f32[1024]{0:T(1024)S(1)}, f32[1024]{0:T(1024)}, u32[]{:S(2)}) copy-start(f32[1024]{0:T(1024)} %param.28) | copy-start | bytes 12292
  122.8 26.3 %copy-start.25 = (f32[1024]{0:T(1024)S(1)}, f32[1024]{0:T(1024)}, u32[]{:S(2)}) copy-start(f32[1024]{0:T(1024)} %param.24) | copy-start | bytes 12292
  122.8 26.3 %copy-start.27 = (f32[2,256]{1,0:T(2,128)S(1)}, f32[2,256]{1,0:T(2,128)}, u32[]{:S(2)}) copy-start(f32[2,256]{1,0:T(2,128)} %param.18) | copy-start | bytes 6148
  122.8 26.3 %copy-start.31 = (f32[1024]{0:T(1024)S(1)}, f32[1024]{0:T(1024)}, u32[]{:S(2)}) copy-start(f32[1024]{0:T(1024)} %param.22) | copy-start | bytes 12292
  149.4 43.9 %copy-start.16 = (bf16[1024,256]{1,0:T(8,128)(2,1)}, bf16[1024,256]{1,0:T(8,128)(2,1)S(1)}, u32[]{:S(2)}) copy-start(bf16[1024,256]{1,0:T(8,128)(2,1)S(1)} %get-tuple-element.1074) | copy-start | bytes 1572868 | tf_op jit(solution)/shard_map/while
  149.4 25.5 %all-gather.14.cloned.1.call-start = ((), (), s32[]{:S(2)}) async-start(), calls=%async_computation.9 | async-start | bytes 2621440 | tf_op jit(solution)/shard_map/while/body/eval_jaxpr/all_gather | solution.py:155
  151.0 90.4 %reduce-scatter.8.cloned.1.call-start = ((), (), s32[]{:S(2)}) async-start(), calls=%async_computation.10 | async-start | bytes 5242880 | tf_op jit(solution)/shard_map/while/body/eval_jaxpr/reduce_scatter | solution.py:169
  196.7 70.3 %all-gather.16.cloned.1.call-start = ((), (), s32[]{:S(2)}) async-start(), calls=%async_computation.11 | async-start | bytes 2621440 | tf_op jit(solution)/shard_map/while/body/eval_jaxpr/all_gather | solution.py:178
  244.2 83.6 %reduce-scatter.12.cloned.1.call-start = ((), (), s32[]{:S(2)}) async-start(), calls=%async_computation.13 | async-start | bytes 5242880 | tf_op jit(solution)/shard_map/while/body/eval_jaxpr/reduce_scatter | solution.py:205
  283.1 71.9 %all-gather.18.cloned.1.call-start = ((), (), s32[]{:S(2)}) async-start(), calls=%async_computation.14 | async-start | bytes 2621440 | tf_op jit(solution)/shard_map/while/body/eval_jaxpr/all_gather | solution.py:216
  332.2 91.2 %reduce-scatter.10.cloned.1.call-start = ((), (), s32[]{:S(2)}) async-start(), calls=%async_computation.12 | async-start | bytes 2621440 | tf_op jit(solution)/shard_map/while/body/eval_jaxpr/reduce_scatter | solution.py:184
  339.4 116.4 %reduce-scatter.14.cloned.1.call-start = ((), (), s32[]{:S(2)}) async-start(), calls=%async_computation.15 | async-start | bytes 5242880 | tf_op jit(solution)/shard_map/while/body/eval_jaxpr/reduce_scatter | solution.py:234
  357.4 12.7 %slice-start.2 = ((s8[8388608]{0:T(1024)(128)(4,1)}), s8[4194304]{0:T(1024)(128)(4,1)S(1)}, s32[]{:S(2)}) async-start(s8[8388608]{0:T(1024)(128)(4,1)} %bitcast.324), calls=%async_computation.18 | async-start | bytes 8388608 | tf_op jit(solution)/shard_map/while
  444.2 15.8 %copy-start.17 = (bf16[1024,256]{1,0:T(8,128)(2,1)S(1)}, bf16[1024,256]{1,0:T(8,128)(2,1)}, u32[]{:S(2)}) copy-start(bf16[1024,256]{1,0:T(8,128)(2,1)} %copy-done.16) | copy-start | bytes 1572868 | tf_op jit(solution)/shard_map/while
  460.2 43.6 %copy-start.16 = (bf16[1024,256]{1,0:T(8,128)(2,1)}, bf16[1024,256]{1,0:T(8,128)(2,1)S(1)}, u32[]{:S(2)}) copy-start(bf16[1024,256]{1,0:T(8,128)(2,1)S(1)} %get-tuple-element.1074) | copy-start | bytes 1572868 | tf_op jit(solution)/shard_map/while
  460.2 25.3 %all-gather.14.cloned.1.call-start = ((), (), s32[]{:S(2)}) async-start(), calls=%async_computation.9 | async-start | bytes 2621440 | tf_op jit(solution)/shard_map/while/body/eval_jaxpr/all_gather | solution.py:155
  461.9 90.1 %reduce-scatter.8.cloned.1.call-start = ((), (), s32[]{:S(2)}) async-start(), calls=%async_computation.10 | async-start | bytes 5242880 | tf_op jit(solution)/shard_map/while/body/eval_jaxpr/reduce_scatter | solution.py:169
  507.2 70.3 %all-gather.16.cloned.1.call-start = ((), (), s32[]{:S(2)}) async-start(), calls=%async_computation.11 | async-start | bytes 2621440 | tf_op jit(solution)/shard_map/while/body/eval_jaxpr/all_gather | solution.py:178
  554.8 83.6 %reduce-scatter.12.cloned.1.call-start = ((), (), s32[]{:S(2)}) async-start(), calls=%async_computation.13 | async-start | bytes 5242880 | tf_op jit(solution)/shard_map/while/body/eval_jaxpr/reduce_scatter | solution.py:205
  593.6 71.9 %all-gather.18.cloned.1.call-start = ((), (), s32[]{:S(2)}) async-start(), calls=%async_computation.14 | async-start | bytes 2621440 | tf_op jit(solution)/shard_map/while/body/eval_jaxpr/all_gather | solution.py:216
  642.8 91.3 %reduce-scatter.10.cloned.1.call-start = ((), (), s32[]{:S(2)}) async-start(), calls=%async_computation.12 | async-start | bytes 2621440 | tf_op jit(solution)/shard_map/while/body/eval_jaxpr/reduce_scatter | solution.py:184
  649.9 116.4 %reduce-scatter.14.cloned.1.call-start = ((), (), s32[]{:S(2)}) async-start(), calls=%async_computation.15 | async-start | bytes 5242880 | tf_op jit(solution)/shard_map/while/body/eval_jaxpr/reduce_scatter | solution.py:234
  668.0 12.7 %slice-start.2 = ((s8[8388608]{0:T(1024)(128)(4,1)}), s8[4194304]{0:T(1024)(128)(4,1)S(1)}, s32[]{:S(2)}) async-start(s8[8388608]{0:T(1024)(128)(4,1)} %bitcast.324), calls=%async_computation.18 | async-start | bytes 8388608 | tf_op jit(solution)/shard_map/while
  772.7 58.8 %all-gather.12.cloned.1.call-start = ((), (), s32[]{:S(2)}) async-start(), calls=%async_computation.8 | async-start | bytes 1622016 | tf_op jit(solution)/shard_map/all_gather | solution.py:279
  773.6 268.2 %reduce-scatter.6.cloned.1.call-start = ((), (), s32[]{:S(2)}) async-start(), calls=%async_computation.7 | async-start | bytes 14155776 | tf_op jit(solution)/shard_map/reduce_scatter | solution.py:267
  (56 other events, 279.1 us)
Sparse Core Ops, SparseCore 0:
  12.6 102.1 all-gather.7
  116.4 32.6 all-gather.9
  152.3 22.5 all-gather.13
  196.8 44.5 reduce-scatter.7
  244.3 22.5 all-gather.15
  283.2 44.5 reduce-scatter.11
  332.4 22.5 all-gather.17
  357.5 31.1 reduce-scatter.9
  410.8 44.8 reduce-scatter.13
  462.9 22.5 all-gather.13
  507.3 44.5 reduce-scatter.7
  554.9 22.5 all-gather.15
  593.8 44.5 reduce-scatter.11
  642.9 22.5 all-gather.17
  667.9 31.1 reduce-scatter.9
  721.4 44.8 reduce-scatter.13
  776.6 54.8 all-gather.11
  834.9 206.8 reduce-scatter.5
